TPU v7x, 512 devices: a whole 4x4x16 slice. The times are simulated.
512 devices in a mesh: leaf: 16 (over z_lo, core), grp: 8 (over y, z_hi), mrg: 4 (over x).
Axes of the slice: x: 4, y: 4, z: 16 (z_hi: 2, z_lo: 8; z = z_hi * 8 + z_lo), core: 2. Of those that a mesh axis runs over, the one named last changes fastest.
Arguments:
- row_owner: int32 [768], replicated, may hold values from 0 to 767, as said below
- face_left: float32 [8, 4, 768, 768], P('grp', 'mrg', 'leaf'), as said below
- face_cross: float32 [8, 4, 768, 768], P('grp', 'mrg', 'leaf')
- face_right: float32 [8, 4, 768, 768], P('grp', 'mrg', 'leaf')
Outputs:
- out_left: float32 [8, 4, 768, 768], P('grp', 'mrg', 'leaf')
- out_cross: float32 [8, 4, 768, 768], P('grp', 'mrg', 'leaf')
- out_right: float32 [8, 4, 768, 768], P('grp', 'mrg', 'leaf')
Inputs may be any that keep to these rules, and one draw needn't show every extreme that they name: row_owner holds each of the 768 face DOFs exactly once. `face_left`: for every box, the symmetric matrix [[L, C], [C^T, R]] built from natural rows is positive definite, L and R are symmetric.
All inputs are finite; a program needn't handle non-finite values.
Results may differ from a plain program's by a relative error of at most 0.0003.
Values sent between devices are 32-bit elements; how exact they have to be, the bound alone decides.
No kernel may reach another device: no remote copies, remote signals or barrier semaphores. Data moves between devices by JAX's collectives and lax.ppermute only.
A program may use at most 128 MiB of HBM per device.

v0:
```python
import jax
import jax.numpy as jnp
from jax import lax
from jax.sharding import PartitionSpec as P


def partner_2(block, axis, distance):
    count = lax.axis_size(axis)
    route = []
    for low in range(count):
        high = low | 1 << distance
        if high != low and high < count:
            route += [(low, high), (high, low)]
    return lax.ppermute(block, axis, route)


def dot_high(left, right):
    return jnp.dot(left, right, precision=lax.Precision.HIGHEST, preferred_element_type=jnp.float32)


def dot_against(left, right):
    return lax.dot_general(
        left,
        right,
        (((1,), (1,)), ((), ())),
        precision=lax.Precision.HIGHEST,
        preferred_element_type=jnp.float32,
    )


def dot_leading(left, right):
    return lax.dot_general(
        left,
        right,
        (((0,), (0,)), ((), ())),
        precision=lax.Precision.HIGHEST,
        preferred_element_type=jnp.float32,
    )


def arrange(mine, partner, role):
    first = jnp.where(role == 0, mine, partner)
    second = jnp.where(role == 0, partner, mine)
    return (first, second)


def merge_rows(first, second, factor, cross_left, cross_right, start):
    rows = first.shape[1]
    columns = lax.dynamic_slice_in_dim(cross_right, start, rows, 1)
    solved = jax.scipy.linalg.cho_solve((factor, True), first[1].T).T
    weights = jax.scipy.linalg.cho_solve((factor, True), columns)
    new_left = first[0] - dot_against(solved, cross_left)
    new_cross = -dot_high(solved, cross_right)
    new_right = second[2] - dot_leading(weights, cross_right)
    return jnp.stack([new_left, new_cross, new_right])


def shards(row_owner, face_left, face_cross, face_right):
    rows = face_left.shape[2]
    width = face_left.shape[3]
    mine = jnp.stack([face_left[0, 0], face_cross[0, 0], face_right[0, 0]])
    mine = jnp.take(mine, row_owner, axis=2)
    inverse_map = (
        jnp.zeros((width,), jnp.int32).at[row_owner].set(jnp.arange(width, dtype=jnp.int32))
    )
    start = lax.axis_index("leaf") * rows
    role_one = lax.axis_index("grp") % 2
    partner = partner_2(mine, "grp", 0)
    first, second = arrange(mine, partner, role_one)
    gathered = lax.all_gather(
        jnp.stack([first[2] + second[0], first[1], second[1]]), "leaf", axis=1, tiled=True
    )
    factor = jnp.linalg.cholesky(gathered[0])
    crossing = gathered[1:]
    mine = merge_rows(first, second, factor, crossing[0], crossing[1], start)
    role_two = lax.axis_index("mrg") % 2
    partner = partner_2(mine, "mrg", 0)
    first, second = arrange(mine, partner, role_two)
    gathered = lax.all_gather(
        jnp.stack([first[2] + second[0], first[1], second[1]]), "leaf", axis=1, tiled=True
    )
    factor = jnp.linalg.cholesky(gathered[0])
    crossing = gathered[1:]
    mine = merge_rows(first, second, factor, crossing[0], crossing[1], start)
    mine = jnp.take(mine, inverse_map, axis=2)
    return (mine[0][None, None], mine[1][None, None], mine[2][None, None])


def solution(mesh):
    in_specs = (
        P(),
        P("grp", "mrg", "leaf", None),
        P("grp", "mrg", "leaf", None),
        P("grp", "mrg", "leaf", None),
    )
    out_specs = (
        P("grp", "mrg", "leaf", None),
        P("grp", "mrg", "leaf", None),
        P("grp", "mrg", "leaf", None),
    )
    return jax.shard_map(shards, mesh=mesh, in_specs=in_specs, out_specs=out_specs, check_vma=False)
```

profile of v0, /device:TPU:4, one launch (start us, length us, event | category | flops | bytes accessed | tf_op | source)
XLA Modules:
  0.0 837.3 jit_solution(3703308753409520388)
XLA Ops:
  10.4 3.4 scatter_custom_fusion
  13.8 2.8 gather_fusion
  17.2 15.7 %collective-permute-start = (f32[3,48,768]{2,1,0:T(8,128)S(1)}, f32[3,48,768]{2,1,0:T(8,128)S(1)}, u32[]{:S(2)}, u32[]{:S(2)}) collective-permute-start(f32[3,48,768]{2,1,0:T(8,128)S(1)} %select_bitcast_fusion.1), channel_id=1, source_target_pairs={{0,4},{4,0},{8,12},{12,8},{16,20},{20,16},{24,28},{28,24},{1,5},{5... | collective-permute-start | bytes 1327112 | tf_op jit(solution)/shard_map/ppermute | solution.py:14
  33.0 14.7 %collective-permute-done = f32[3,48,768]{2,1,0:T(8,128)S(1)} collective-permute-done((f32[3,48,768]{2,1,0:T(8,128)S(1)}, f32[3,48,768]{2,1,0:T(8,128)S(1)}, u32[]{:S(2)}, u32[]{:S(2)}) %collective-permute-start) | collective-permute-done | bytes 442400 | tf_op jit(solution)/shard_map/ppermute | solution.py:14
  49.6 138.4 %all-gather.3.cloned.1.call-done = f32[3,768,768]{2,1,0:T(8,128)} async-done(((f32[3,48,768]{2,1,0:T(8,128)}), f32[3,768,768]{2,1,0:T(8,128)}) %all-gather.3.cloned.1.call-update) | async-done | bytes 7077904 | tf_op jit(solution)/shard_map/all_gather | solution.py:70
  188.0 4.1 fusion.325
  198.7 11.7 %cholesky.453 = f32[128,128]{1,0:T(8,128)S(1)} custom-call(f32[128,128]{1,0:T(8,128)S(1)} %cholesky.669), custom_call_target="Cholesky" | custom-call | tf_op jit(solution)/shard_map/jit(cholesky)/cholesky | solution.py:73
  210.6 9.8 %custom-call.45 = f32[1,128,128]{1,2,0:T(8,128)S(1)} custom-call(f32[1,128,128]{2,1,0:T(8,128)S(1)} %get-tuple-element.115), custom_call_target="InvertDiagBlocksLowerTriangular" | custom-call | tf_op jit(solution)/shard_map/jit(cholesky)/cholesky | solution.py:73
  223.3 11.7 %cholesky.472 = f32[128,128]{1,0:T(8,128)S(1)} custom-call(f32[128,128]{1,0:T(8,128)S(1)} %cholesky.673), custom_call_target="Cholesky" | custom-call | tf_op jit(solution)/shard_map/jit(cholesky)/cholesky | solution.py:73
  235.0 10.0 %custom-call.46 = f32[1,128,128]{1,2,0:T(8,128)S(1)} custom-call(f32[1,128,128]{2,1,0:T(8,128)S(1)} %get-tuple-element.112), custom_call_target="InvertDiagBlocksLowerTriangular" | custom-call | tf_op jit(solution)/shard_map/jit(cholesky)/cholesky | solution.py:73
  247.0 11.7 %cholesky.493 = f32[128,128]{1,0:T(8,128)S(1)} custom-call(f32[128,128]{1,0:T(8,128)S(1)} %cholesky.678), custom_call_target="Cholesky" | custom-call | tf_op jit(solution)/shard_map/jit(cholesky)/cholesky | solution.py:73
  258.7 9.8 %custom-call.47 = f32[1,128,128]{1,2,0:T(8,128)S(1)} custom-call(f32[1,128,128]{2,1,0:T(8,128)S(1)} %get-tuple-element.109), custom_call_target="InvertDiagBlocksLowerTriangular" | custom-call | tf_op jit(solution)/shard_map/jit(cholesky)/cholesky | solution.py:73
  270.4 12.2 %cholesky.512 = f32[128,128]{1,0:T(8,128)S(1)} custom-call(f32[128,128]{1,0:T(8,128)S(1)} %cholesky.683), custom_call_target="Cholesky" | custom-call | tf_op jit(solution)/shard_map/jit(cholesky)/cholesky | solution.py:73
  282.6 9.8 %custom-call.48 = f32[1,128,128]{1,2,0:T(8,128)S(1)} custom-call(f32[1,128,128]{2,1,0:T(8,128)S(1)} %get-tuple-element.106), custom_call_target="InvertDiagBlocksLowerTriangular" | custom-call | tf_op jit(solution)/shard_map/jit(cholesky)/cholesky | solution.py:73
  294.2 11.7 %cholesky.531 = f32[128,128]{1,0:T(8,128)S(1)} custom-call(f32[128,128]{1,0:T(8,128)S(1)} %cholesky.688), custom_call_target="Cholesky" | custom-call | tf_op jit(solution)/shard_map/jit(cholesky)/cholesky | solution.py:73
  305.9 9.8 %custom-call.49 = f32[1,128,128]{1,2,0:T(8,128)S(1)} custom-call(f32[1,128,128]{2,1,0:T(8,128)S(1)} %get-tuple-element.103), custom_call_target="InvertDiagBlocksLowerTriangular" | custom-call | tf_op jit(solution)/shard_map/jit(cholesky)/cholesky | solution.py:73
  317.3 11.9 %cholesky.548 = f32[128,128]{1,0:T(8,128)S(1)} custom-call(f32[128,128]{1,0:T(8,128)S(1)} %convolution_subtract_fusion.9), custom_call_target="Cholesky" | custom-call | tf_op jit(solution)/shard_map/jit(cholesky)/cholesky | solution.py:73
  337.2 3.4 select_select_fusion.1
  340.6 17.9 %while.8 = (s32[]{:T(128)}, f32[768,768]{1,0:T(8,128)}, s32[6,2]{0,1:T(2,128)S(1)}, f32[6,128,128]{2,1,0:T(8,128)S(1)}, s32[]{:T(128)}) while((s32[]{:T(128)}, f32[768,768]{1,0:T(8,128)}, s32[6,2]{0,1:T(2,128)S(1)}, f32[6,128,128]{2,1,0:T(8,128)S(1)}, s32[]{:T(128)}) %tuple.109), condition=%wide.while_cond, body=%wide.while_body.sunk | while | flops 2 | bytes 131189 | solution.py:50
  359.3 59.8 %custom-call.50 = f32[6,128,128]{1,2,0:T(8,128)S(1)} custom-call(f32[6,128,128]{2,1,0:T(8,128)} %copy-done.11), custom_call_target="InvertDiagBlocksLowerTriangular" | custom-call | tf_op jit(solution)/shard_map/jit(_cho_solve)/triangular_solve | solution.py:50
  437.5 3.2 fusion.81
  440.7 2.4 fusion.79
  443.2 2.7 collective-permute-start.1
  445.9 7.4 collective-permute-done.1
  455.2 109.9 %all-gather.5.cloned.1.call-done = f32[3,768,768]{2,1,0:T(8,128)} async-done(((f32[3,48,768]{2,1,0:T(8,128)}), f32[3,768,768]{2,1,0:T(8,128)}) %all-gather.5.cloned.1.call-update) | async-done | bytes 7077904 | tf_op jit(solution)/shard_map/all_gather | solution.py:79
  565.2 4.1 fusion.324
  570.3 2.4 copy.47
  576.2 11.7 %cholesky.563 = f32[128,128]{1,0:T(8,128)S(1)} custom-call(f32[128,128]{1,0:T(8,128)S(1)} %cholesky.692), custom_call_target="Cholesky" | custom-call | tf_op jit(solution)/shard_map/jit(cholesky)/cholesky | solution.py:82
  588.1 9.8 %custom-call.52 = f32[1,128,128]{1,2,0:T(8,128)S(1)} custom-call(f32[1,128,128]{2,1,0:T(8,128)S(1)} %get-tuple-element.99), custom_call_target="InvertDiagBlocksLowerTriangular" | custom-call | tf_op jit(solution)/shard_map/jit(cholesky)/cholesky | solution.py:82
  600.7 11.7 %cholesky.582 = f32[128,128]{1,0:T(8,128)S(1)} custom-call(f32[128,128]{1,0:T(8,128)S(1)} %cholesky.696), custom_call_target="Cholesky" | custom-call | tf_op jit(solution)/shard_map/jit(cholesky)/cholesky | solution.py:82
  612.4 10.0 %custom-call.53 = f32[1,128,128]{1,2,0:T(8,128)S(1)} custom-call(f32[1,128,128]{2,1,0:T(8,128)S(1)} %get-tuple-element.96), custom_call_target="InvertDiagBlocksLowerTriangular" | custom-call | tf_op jit(solution)/shard_map/jit(cholesky)/cholesky | solution.py:82
  624.3 11.7 %cholesky.603 = f32[128,128]{1,0:T(8,128)S(1)} custom-call(f32[128,128]{1,0:T(8,128)S(1)} %cholesky.701), custom_call_target="Cholesky" | custom-call | tf_op jit(solution)/shard_map/jit(cholesky)/cholesky | solution.py:82
  636.1 9.8 %custom-call.54 = f32[1,128,128]{1,2,0:T(8,128)S(1)} custom-call(f32[1,128,128]{2,1,0:T(8,128)S(1)} %get-tuple-element.93), custom_call_target="InvertDiagBlocksLowerTriangular" | custom-call | tf_op jit(solution)/shard_map/jit(cholesky)/cholesky | solution.py:82
  647.8 12.1 %cholesky.622 = f32[128,128]{1,0:T(8,128)S(1)} custom-call(f32[128,128]{1,0:T(8,128)S(1)} %cholesky.706), custom_call_target="Cholesky" | custom-call | tf_op jit(solution)/shard_map/jit(cholesky)/cholesky | solution.py:82
  659.9 9.8 %custom-call.55 = f32[1,128,128]{1,2,0:T(8,128)S(1)} custom-call(f32[1,128,128]{2,1,0:T(8,128)S(1)} %get-tuple-element.90), custom_call_target="InvertDiagBlocksLowerTriangular" | custom-call | tf_op jit(solution)/shard_map/jit(cholesky)/cholesky | solution.py:82
  671.5 11.7 %cholesky.641 = f32[128,128]{1,0:T(8,128)S(1)} custom-call(f32[128,128]{1,0:T(8,128)S(1)} %cholesky.711), custom_call_target="Cholesky" | custom-call | tf_op jit(solution)/shard_map/jit(cholesky)/cholesky | solution.py:82
  683.3 9.8 %custom-call.56 = f32[1,128,128]{1,2,0:T(8,128)S(1)} custom-call(f32[1,128,128]{2,1,0:T(8,128)S(1)} %get-tuple-element.87), custom_call_target="InvertDiagBlocksLowerTriangular" | custom-call | tf_op jit(solution)/shard_map/jit(cholesky)/cholesky | solution.py:82
  694.6 11.7 %cholesky.658 = f32[128,128]{1,0:T(8,128)S(1)} custom-call(f32[128,128]{1,0:T(8,128)S(1)} %convolution_subtract_fusion.8), custom_call_target="Cholesky" | custom-call | tf_op jit(solution)/shard_map/jit(cholesky)/cholesky | solution.py:82
  714.4 3.4 select_select_fusion
  717.8 18.1 %while.9 = (s32[]{:T(128)}, f32[768,768]{1,0:T(8,128)}, s32[6,2]{0,1:T(2,128)S(1)}, f32[6,128,128]{2,1,0:T(8,128)S(1)}, s32[]{:T(128)}) while((s32[]{:T(128)}, f32[768,768]{1,0:T(8,128)}, s32[6,2]{0,1:T(2,128)S(1)}, f32[6,128,128]{2,1,0:T(8,128)S(1)}, s32[]{:T(128)}) %tuple.119), condition=%wide.while_cond.clone.1, body=%wide.while_body.clone.1.sunk | while | flops 2 | bytes 131189 | solution.py:50
  718.5 2.3 bitcast_dynamic-update-slice_fusion.5
  721.5 2.3 bitcast_dynamic-update-slice_fusion.5
  724.5 2.3 bitcast_dynamic-update-slice_fusion.5
  736.6 59.9 %custom-call.57 = f32[6,128,128]{1,2,0:T(8,128)S(1)} custom-call(f32[6,128,128]{2,1,0:T(8,128)} %copy-done.10), custom_call_target="InvertDiagBlocksLowerTriangular" | custom-call | tf_op jit(solution)/shard_map/jit(_cho_solve)/triangular_solve | solution.py:50
  815.0 3.2 fusion.77
  818.2 2.4 fusion.75
  821.4 2.8 gather_fusion.1
  824.2 2.8 select_bitcast_fusion
  (287 shorter events, 117.3 us)
Async XLA Ops:
  7.2 180.8 %all-gather.3.cloned.1.call-start = ((), (), s32[]{:S(2)}) async-start(), calls=%async_computation | async-start | bytes 7520256 | tf_op jit(solution)/shard_map/all_gather | solution.py:70
  17.2 30.4 %collective-permute-start = (f32[3,48,768]{2,1,0:T(8,128)S(1)}, f32[3,48,768]{2,1,0:T(8,128)S(1)}, u32[]{:S(2)}, u32[]{:S(2)}) collective-permute-start(f32[3,48,768]{2,1,0:T(8,128)S(1)} %select_bitcast_fusion.1), channel_id=1, source_target_pairs={{0,4},{4,0},{8,12},{12,8},{16,20},{20,16},{24,28},{28,24},{1,5},{5... | collective-permute-start | bytes 1327112 | tf_op jit(solution)/shard_map/ppermute | solution.py:14
  47.8 0.8 copy-start.6
  47.8 0.9 copy-start.7
  49.5 515.6 %all-gather.5.cloned.1.call-start = ((), (), s32[]{:S(2)}) async-start(), calls=%async_computation.1 | async-start | bytes 7520256 | tf_op jit(solution)/shard_map/all_gather | solution.py:79
  197.3 1.5 copy-start.4
  329.2 8.0 copy-start
  337.2 98.8 %slice-start = ((s8[7077888]{0:T(1024)(128)(4,1)}), s8[2883584]{0:T(1024)(128)(4,1)S(1)}, s32[]{:S(2)}) async-start(s8[7077888]{0:T(1024)(128)(4,1)} %bitcast.376), calls=%async_computation.2 | async-start | bytes 5767168
  358.5 0.7 copy-start.11
  419.0 8.8 %copy-start.3 = (f32[768,768]{1,0:T(8,128)S(1)}, f32[768,768]{1,0:T(8,128)}, u32[]{:S(2)}) copy-start(f32[768,768]{1,0:T(8,128)} %get-tuple-element.263) | copy-start | bytes 7077892
  425.7 10.2 %slice-start.1 = ((s8[7077888]{0:T(1024)(128)(4,1)}), s8[4194304]{0:T(1024)(128)(4,1)S(1)}, s32[]{:S(2)}) async-start(s8[7077888]{0:T(1024)(128)(4,1)} %bitcast.376), calls=%async_computation.3 | async-start | bytes 8388608
  443.2 10.2 %collective-permute-start.1 = (f32[3,48,768]{2,1,0:T(8,128)S(1)}, f32[3,48,768]{2,1,0:T(8,128)S(1)}, u32[]{:S(2)}, u32[]{:S(2)}) collective-permute-start(f32[3,48,768]{2,1,0:T(8,128)S(1)} %pad_maximum_fusion.2), channel_id=1, source_target_pairs={{0,1},{1,0},{2,3},{3,2},{4,5},{5,4},{6,7},{7,6},{8,9},{9,8},{10,11... | collective-permute-start | bytes 1327112 | tf_op jit(solution)/shard_map/ppermute | solution.py:14
  453.4 0.8 copy-start.8
  453.4 0.9 copy-start.9
  574.7 1.5 copy-start.5
  706.4 8.0 copy-start.1
  714.3 99.2 %slice-start.2 = ((s8[7077888]{0:T(1024)(128)(4,1)}), s8[2883584]{0:T(1024)(128)(4,1)S(1)}, s32[]{:S(2)}) async-start(s8[7077888]{0:T(1024)(128)(4,1)} %bitcast.378), calls=%async_computation.4 | async-start | bytes 5767168
  735.9 0.7 copy-start.10
  796.6 8.7 %copy-start.2 = (f32[768,768]{1,0:T(8,128)S(1)}, f32[768,768]{1,0:T(8,128)}, u32[]{:S(2)}) copy-start(f32[768,768]{1,0:T(8,128)} %get-tuple-element.262) | copy-start | bytes 7077892
  803.3 10.2 %slice-start.3 = ((s8[7077888]{0:T(1024)(128)(4,1)}), s8[4194304]{0:T(1024)(128)(4,1)S(1)}, s32[]{:S(2)}) async-start(s8[7077888]{0:T(1024)(128)(4,1)} %bitcast.378), calls=%async_computation.5 | async-start | bytes 8388608
Sparse Core Ops, SparseCore 0:
  49.6 138.2 all-gather.2
  455.3 109.7 all-gather.4
where the time goes:
time: 842 us; the launch traced here: 837 us
  other arithmetic  386 us (46%)
  waiting for transfers between devices  270 us (32%)
  local copies, waits for them, and re-layouts  71.6 us (9%)
  matrix products  66.5 us (8%)
  between operations  23.6 us (3%)
  starting transfers between devices  18.6 us (2%)
    another operation x46, other arithmetic, shards(): factor = jnp.linalg.cholesky(gathered[0])  249 us
    all_gather x2, waiting for transfers between devices, shards(): lax.all_gather(jnp.stack([first[2] + second[0], first[1], second[1]]), 'l...  248 us
    another operation x5, other arithmetic, merge_rows(): solved = jax.scipy.linalg.cho_solve((factor, True), first[1].T).T  126 us
    another operation x43, local copies, waits for them, and re-layouts, merge_rows(): solved = jax.scipy.linalg.cho_solve((factor, True), first[1].T).T  35.8 us
    ppermute x2, waiting for transfers between devices, partner_2(): return lax.ppermute(block, axis, route)  22.1 us
    another operation x44, matrix products, merge_rows(): weights = jax.scipy.linalg.cho_solve((factor, True), columns)  22 us
    another operation x20, matrix products, shards(): factor = jnp.linalg.cholesky(gathered[0])  19.6 us
    ppermute x2, starting transfers between devices, partner_2(): return lax.ppermute(block, axis, route)  18.5 us
  transfers between devices with their start and end apart: 4, of which 4 were waited for; matrix products, arithmetic and copies ran while one was open for 0% of the time, Pallas kernels for 0%

commit v1 on v0

--- a/solution.py
+++ b/solution.py
@@ -67,9 +67,11 @@
     role_one = lax.axis_index("grp") % 2
     partner = partner_2(mine, "grp", 0)
     first, second = arrange(mine, partner, role_one)
-    gathered = lax.all_gather(
-        jnp.stack([first[2] + second[0], first[1], second[1]]), "leaf", axis=1, tiled=True
-    )
+    block_2 = jnp.stack([first[2] + second[0], first[1], second[1]])
+    peers = lax.axis_size("leaf")
+    parts = jnp.stack([block_2 for _ in range(peers)])
+    parts = lax.all_to_all(parts, "leaf", split_axis=0, concat_axis=0)
+    gathered = jnp.concatenate(parts, axis=1)
     factor = jnp.linalg.cholesky(gathered[0])
     crossing = gathered[1:]
     mine = merge_rows(first, second, factor, crossing[0], crossing[1], start)

time: 842 us -> 1060 us (1.26)
  waiting for transfers between devices: 270 us -> 445 us
  starting transfers between devices: 18.6 us -> 50.1 us
    all_to_all x0 -> x1, waiting for transfers between devices: none -> 254 us  [shards(): parts = lax.all_to_all(parts, 'leaf', split_axis=0, concat_axis=0)]
    all_gather x2 -> x1, waiting for transfers between devices: 248 us -> 165 us  [shards(): lax.all_gather(jnp.stack([first[2] + second[0], first[1], second[1]]), 'l...]
    all_to_all x0 -> x1, starting transfers between devices: none -> 31.2 us  [shards(): parts = lax.all_to_all(parts, 'leaf', split_axis=0, concat_axis=0)]
where the time goes in v1:
time: 1060 us
  waiting for transfers between devices  445 us (42%)
  other arithmetic  391 us (37%)
  local copies, waits for them, and re-layouts  77.1 us (7%)
  matrix products  72.6 us (7%)
  starting transfers between devices  50.1 us (5%)
  between operations  23.2 us (2%)
    all_to_all x1, waiting for transfers between devices, shards(): parts = lax.all_to_all(parts, 'leaf', split_axis=0, concat_axis=0)  254 us
    another operation x46, other arithmetic, shards(): factor = jnp.linalg.cholesky(gathered[0])  251 us
    all_gather x1, waiting for transfers between devices, shards(): lax.all_gather(jnp.stack([first[2] + second[0], first[1], second[1]]), 'l...  165 us
    another operation x5, other arithmetic, merge_rows(): solved = jax.scipy.linalg.cho_solve((factor, True), first[1].T).T  127 us
    another operation x43, local copies, waits for them, and re-layouts, merge_rows(): solved = jax.scipy.linalg.cho_solve((factor, True), first[1].T).T  34.1 us
    all_to_all x1, starting transfers between devices, shards(): parts = lax.all_to_all(parts, 'leaf', split_axis=0, concat_axis=0)  31.2 us
    ppermute x2, waiting for transfers between devices, partner_2(): return lax.ppermute(block, axis, route)  26.5 us
    another operation x44, matrix products, merge_rows(): weights = jax.scipy.linalg.cho_solve((factor, True), columns)  24.4 us
  transfers between devices with their start and end apart: 4, of which 4 were waited for; matrix products, arithmetic and copies ran while one was open for 0% of the time, Pallas kernels for 0%

profile of v1, /device:TPU:4, one launch (start us, length us, event | category | flops | bytes accessed | tf_op | source)
XLA Modules:
  0.0 1059.0 jit_solution(5296946560435429019)
XLA Ops:
  10.4 3.4 scatter_custom_fusion
  14.3 2.8 gather_fusion
  17.8 15.7 %collective-permute-start = (f32[3,48,768]{2,1,0:T(8,128)S(1)}, f32[3,48,768]{2,1,0:T(8,128)S(1)}, u32[]{:S(2)}, u32[]{:S(2)}) collective-permute-start(f32[3,48,768]{2,1,0:T(8,128)S(1)} %select_bitcast_fusion.1), channel_id=1, source_target_pairs={{0,4},{4,0},{8,12},{12,8},{16,20},{20,16},{24,28},{28,24},{1,5},{5... | collective-permute-start | bytes 1327112 | tf_op jit(solution)/shard_map/ppermute | solution.py:14
  33.5 14.7 %collective-permute-done = f32[3,48,768]{2,1,0:T(8,128)S(1)} collective-permute-done((f32[3,48,768]{2,1,0:T(8,128)S(1)}, f32[3,48,768]{2,1,0:T(8,128)S(1)}, u32[]{:S(2)}, u32[]{:S(2)}) %collective-permute-start) | collective-permute-done | bytes 442400 | tf_op jit(solution)/shard_map/ppermute | solution.py:14
  49.1 3.8 stack.26
  52.9 31.2 %all-to-all-start = ((f32[16,3,48,768]{3,2,1,0:T(8,128)}), f32[16,3,48,768]{3,2,1,0:T(8,128)}, u32[]{:S(2)}, u32[]{:S(2)}) async-start(f32[16,3,48,768]{3,2,1,0:T(8,128)} %stack.26), calls=%async_computation | async-start | bytes 14155776 | tf_op jit(solution)/shard_map/all_to_all | solution.py:73
  84.8 253.6 %all-to-all-done = f32[16,3,48,768]{3,2,1,0:T(8,128)} async-done(((f32[16,3,48,768]{3,2,1,0:T(8,128)}), f32[16,3,48,768]{3,2,1,0:T(8,128)}, u32[]{:S(2)}, u32[]{:S(2)}) %all-to-all-start) | async-done | bytes 7077920 | tf_op jit(solution)/shard_map/all_to_all | solution.py:73
  338.4 3.5 copy.57
  341.8 2.6 fusion.312
  344.4 3.2 copy.38
  347.6 2.7 fusion.6
  351.7 11.7 %cholesky.453 = f32[128,128]{1,0:T(8,128)S(1)} custom-call(f32[128,128]{1,0:T(8,128)S(1)} %cholesky.669), custom_call_target="Cholesky" | custom-call | tf_op jit(solution)/shard_map/jit(cholesky)/cholesky | solution.py:75
  365.1 9.8 custom-call.45
  378.5 11.7 %cholesky.472 = f32[128,128]{1,0:T(8,128)S(1)} custom-call(f32[128,128]{1,0:T(8,128)S(1)} %cholesky.673), custom_call_target="Cholesky" | custom-call | tf_op jit(solution)/shard_map/jit(cholesky)/cholesky | solution.py:75
  390.8 10.2 custom-call.46
  403.9 11.7 %cholesky.493 = f32[128,128]{1,0:T(8,128)S(1)} custom-call(f32[128,128]{1,0:T(8,128)S(1)} %cholesky.678), custom_call_target="Cholesky" | custom-call | tf_op jit(solution)/shard_map/jit(cholesky)/cholesky | solution.py:75
  416.3 9.8 custom-call.47
  429.0 11.9 %cholesky.512 = f32[128,128]{1,0:T(8,128)S(1)} custom-call(f32[128,128]{1,0:T(8,128)S(1)} %cholesky.683), custom_call_target="Cholesky" | custom-call | tf_op jit(solution)/shard_map/jit(cholesky)/cholesky | solution.py:75
  441.5 9.8 custom-call.48
  454.0 11.7 %cholesky.531 = f32[128,128]{1,0:T(8,128)S(1)} custom-call(f32[128,128]{1,0:T(8,128)S(1)} %cholesky.688), custom_call_target="Cholesky" | custom-call | tf_op jit(solution)/shard_map/jit(cholesky)/cholesky | solution.py:75
  466.3 9.8 custom-call.49
  478.6 11.7 %cholesky.548 = f32[128,128]{1,0:T(8,128)S(1)} custom-call(f32[128,128]{1,0:T(8,128)S(1)} %convolution_subtract_fusion.9), custom_call_target="Cholesky" | custom-call | tf_op jit(solution)/shard_map/jit(cholesky)/cholesky | solution.py:75
  498.6 3.3 select_select_fusion.1
  501.9 16.9 %while.8 = (s32[]{:T(128)}, f32[768,768]{1,0:T(8,128)}, s32[6,2]{0,1:T(2,128)S(1)}, f32[6,128,128]{2,1,0:T(8,128)S(1)}, s32[]{:T(128)}) while((s32[]{:T(128)}, f32[768,768]{1,0:T(8,128)}, s32[6,2]{0,1:T(2,128)S(1)}, f32[6,128,128]{2,1,0:T(8,128)S(1)}, s32[]{:T(128)}) %tuple.114), condition=%wide.while_cond, body=%wide.while_body.sunk | while | flops 2 | bytes 131189 | solution.py:50
  519.5 60.2 %custom-call.50 = f32[6,128,128]{1,2,0:T(8,128)S(1)} custom-call(f32[6,128,128]{2,1,0:T(8,128)} %copy-done.11), custom_call_target="InvertDiagBlocksLowerTriangular" | custom-call | tf_op jit(solution)/shard_map/jit(_cho_solve)/triangular_solve | solution.py:50
  594.5 2.4 fusion.69
  606.4 3.1 collective-permute-start.1
  609.5 11.8 %collective-permute-done.1 = f32[3,48,768]{2,1,0:T(8,128)S(1)} collective-permute-done((f32[3,48,768]{2,1,0:T(8,128)S(1)}, f32[3,48,768]{2,1,0:T(8,128)S(1)}, u32[]{:S(2)}, u32[]{:S(2)}) %collective-permute-start.1) | collective-permute-done | bytes 442400 | tf_op jit(solution)/shard_map/ppermute | solution.py:14
  623.2 164.9 %all-gather.2.cloned.1.call-done = f32[3,768,768]{2,1,0:T(8,128)} async-done(((f32[3,48,768]{2,1,0:T(8,128)}), f32[3,768,768]{2,1,0:T(8,128)}) %all-gather.2.cloned.1.call-update) | async-done | bytes 7077904 | tf_op jit(solution)/shard_map/all_gather | solution.py:81
  788.1 4.1 fusion.311
  798.9 11.7 %cholesky.563 = f32[128,128]{1,0:T(8,128)S(1)} custom-call(f32[128,128]{1,0:T(8,128)S(1)} %cholesky.692), custom_call_target="Cholesky" | custom-call | tf_op jit(solution)/shard_map/jit(cholesky)/cholesky | solution.py:84
  810.8 9.8 custom-call.52
  823.4 11.7 %cholesky.582 = f32[128,128]{1,0:T(8,128)S(1)} custom-call(f32[128,128]{1,0:T(8,128)S(1)} %cholesky.696), custom_call_target="Cholesky" | custom-call | tf_op jit(solution)/shard_map/jit(cholesky)/cholesky | solution.py:84
  835.2 10.2 custom-call.53
  847.3 11.7 %cholesky.603 = f32[128,128]{1,0:T(8,128)S(1)} custom-call(f32[128,128]{1,0:T(8,128)S(1)} %cholesky.701), custom_call_target="Cholesky" | custom-call | tf_op jit(solution)/shard_map/jit(cholesky)/cholesky | solution.py:84
  859.0 9.8 custom-call.54
  870.7 11.9 %cholesky.622 = f32[128,128]{1,0:T(8,128)S(1)} custom-call(f32[128,128]{1,0:T(8,128)S(1)} %cholesky.706), custom_call_target="Cholesky" | custom-call | tf_op jit(solution)/shard_map/jit(cholesky)/cholesky | solution.py:84
  882.7 9.8 custom-call.55
  894.2 11.7 %cholesky.641 = f32[128,128]{1,0:T(8,128)S(1)} custom-call(f32[128,128]{1,0:T(8,128)S(1)} %cholesky.711), custom_call_target="Cholesky" | custom-call | tf_op jit(solution)/shard_map/jit(cholesky)/cholesky | solution.py:84
  906.0 9.8 custom-call.56
  917.3 11.7 %cholesky.658 = f32[128,128]{1,0:T(8,128)S(1)} custom-call(f32[128,128]{1,0:T(8,128)S(1)} %convolution_subtract_fusion.8), custom_call_target="Cholesky" | custom-call | tf_op jit(solution)/shard_map/jit(cholesky)/cholesky | solution.py:84
  936.6 3.5 select_select_fusion
  940.1 17.4 %while.9 = (s32[]{:T(128)}, f32[768,768]{1,0:T(8,128)}, s32[6,2]{0,1:T(2,128)S(1)}, f32[6,128,128]{2,1,0:T(8,128)S(1)}, s32[]{:T(128)}) while((s32[]{:T(128)}, f32[768,768]{1,0:T(8,128)}, s32[6,2]{0,1:T(2,128)S(1)}, f32[6,128,128]{2,1,0:T(8,128)S(1)}, s32[]{:T(128)}) %tuple.122), condition=%wide.while_cond.clone.1, body=%wide.while_body.clone.1.sunk | while | flops 2 | bytes 131189 | solution.py:50
  958.3 60.0 %custom-call.57 = f32[6,128,128]{1,2,0:T(8,128)S(1)} custom-call(f32[6,128,128]{2,1,0:T(8,128)} %copy-done.10), custom_call_target="InvertDiagBlocksLowerTriangular" | custom-call | tf_op jit(solution)/shard_map/jit(_cho_solve)/triangular_solve | solution.py:50
  1036.7 3.2 fusion.67
  1039.9 2.4 fusion.65
  1043.1 2.8 gather_fusion.1
  1046.0 2.8 select_bitcast_fusion
  (291 shorter events, 134.3 us)
Async XLA Ops:
  17.8 30.4 %collective-permute-start = (f32[3,48,768]{2,1,0:T(8,128)S(1)}, f32[3,48,768]{2,1,0:T(8,128)S(1)}, u32[]{:S(2)}, u32[]{:S(2)}) collective-permute-start(f32[3,48,768]{2,1,0:T(8,128)S(1)} %select_bitcast_fusion.1), channel_id=1, source_target_pairs={{0,4},{4,0},{8,12},{12,8},{16,20},{20,16},{24,28},{28,24},{1,5},{5... | collective-permute-start | bytes 1327112 | tf_op jit(solution)/shard_map/ppermute | solution.py:14
  48.3 4.6 copy-start.6
  52.9 285.5 %all-to-all-start = ((f32[16,3,48,768]{3,2,1,0:T(8,128)}), f32[16,3,48,768]{3,2,1,0:T(8,128)}, u32[]{:S(2)}, u32[]{:S(2)}) async-start(f32[16,3,48,768]{3,2,1,0:T(8,128)} %stack.26), calls=%async_computation | async-start | bytes 14155776 | tf_op jit(solution)/shard_map/all_to_all | solution.py:73
  84.1 704.0 %all-gather.2.cloned.1.call-start = ((), (), s32[]{:S(2)}) async-start(), calls=%async_computation.1 | async-start | bytes 7520256 | tf_op jit(solution)/shard_map/all_gather | solution.py:81
  350.3 1.4 copy-start.4
  498.6 3.3 copy-start.13
  518.8 0.8 copy-start.11
  581.8 10.1 copy-start.1
  592.8 4.1 copy-start.9
  600.8 3.2 copy-start.3
  606.4 14.9 %collective-permute-start.1 = (f32[3,48,768]{2,1,0:T(8,128)S(1)}, f32[3,48,768]{2,1,0:T(8,128)S(1)}, u32[]{:S(2)}, u32[]{:S(2)}) collective-permute-start(f32[3,48,768]{2,1,0:T(8,128)S(1)} %pad_maximum_fusion.2), channel_id=1, source_target_pairs={{0,1},{1,0},{2,3},{3,2},{4,5},{5,4},{6,7},{7,6},{8,9},{9,8},{10,11... | collective-permute-start | bytes 1327112 | tf_op jit(solution)/shard_map/ppermute | solution.py:14
  621.4 0.8 copy-start.7
  621.4 0.9 copy-start.8
  797.4 1.5 copy-start.5
  929.1 7.5 copy-start
  936.6 98.6 %slice-start = ((s8[7077888]{0:T(1024)(128)(4,1)}), s8[2883584]{0:T(1024)(128)(4,1)S(1)}, s32[]{:S(2)}) async-start(s8[7077888]{0:T(1024)(128)(4,1)} %bitcast.366), calls=%async_computation.2 | async-start | bytes 5767168
  957.5 0.7 copy-start.10
  1018.2 8.7 copy-start.2
  1025.0 10.2 slice-start.1
  1039.9 3.2 copy-start.12
Sparse Core Ops, SparseCore 0:
  623.3 164.7 all-gather.1
